TPU v7x, 256 devices: a whole 4x4x8 slice. The times are simulated.
256 devices in a mesh: layer: 4 (over y), rep: 2 (over core), row: 4 (over x), col: 8 (over z).
Axes of the slice: x: 4, y: 4, z: 8, core: 2. Of those that a mesh axis runs over, the one named last changes fastest.
Arguments:
- iterate: bfloat16 [14336, 8192], P(('layer', 'row'), ('rep', 'col')), parts along dimension 0, may hold values from -0.03125 to 0.03125
Outputs:
- next_iterate: bfloat16 [14336, 8192], P(('layer', 'row'), ('rep', 'col')), parts along dimension 0
There are 4 independent parts, one for each index of `layer`. A program takes and returns all parts, laid end to end along the dimension named above; each array names one. Nothing has to cross between parts.
All inputs are finite; a program needn't handle non-finite values.
Results may differ from a plain program's by a relative error of at most 0.017.
Values may be sent and summed in bfloat16 or wider, within the bound.
A program may use at most 64 MiB of HBM per device.

v0:
```python
import jax
import jax.numpy as jnp
from jax import lax
from jax.sharding import PartitionSpec as P

COLS = 8192


coef_linear = 3.4445
coef_cubic = -4.775
coef_quintic = 2.0315


def summed_rows(terms, axes):
    total = terms.astype(jnp.bfloat16)
    for axis in axes:
        total = lax.psum_scatter(total, axis, scatter_dimension=0, tiled=True)
    return total.astype(jnp.float32)


def in_order(tiles, dim):
    shape = list(tiles.shape[1:])
    shape[dim] *= tiles.shape[0]
    return jnp.moveaxis(tiles, 0, dim).reshape(shape)


def from_everyone(x, axis):
    copies = jnp.broadcast_to(x, (lax.axis_size(axis), *x.shape))
    return lax.all_to_all(copies, axis, split_axis=0, concat_axis=0, tiled=True)


def gather_directly(x, axis, dim):
    return in_order(from_everyone(x, axis), dim)


def contract_first(left_side, right_side):
    return lax.dot_general(
        left_side, right_side, (((0,), (0,)), ((), ())), preferred_element_type=jnp.float32
    )


def local(iterate):
    column_panel = lax.all_gather(iterate, "row", axis=0, tiled=True)
    panel_rows = column_panel
    gram_tile = summed_rows(
        lax.dot_general(
            panel_rows, iterate, (((1,), (1,)), ((), ())), preferred_element_type=jnp.float32
        ),
        ("rep", "col"),
    ).astype(jnp.bfloat16)
    gram_band = gather_directly(gram_tile, "row", 1)
    square_tile = summed_rows(contract_first(gram_band, gram_tile), ("rep", "col"))
    combo_tile = (coef_cubic * gram_tile.astype(jnp.float32) + coef_quintic * square_tile).astype(
        jnp.bfloat16
    )
    panel_rows = column_panel
    product = contract_first(
        lax.all_gather(combo_tile, ("rep", "col"), axis=0, tiled=True), panel_rows
    )
    scale_factor = 0.2 * jnp.sqrt(jnp.float32(COLS))
    return (scale_factor * (coef_linear * iterate.astype(jnp.float32) + product)).astype(
        jnp.bfloat16
    )


def solution(mesh):
    in_specs = (P(("layer", "row"), ("rep", "col")),)
    out_specs = P(("layer", "row"), ("rep", "col"))
    return jax.shard_map(local, mesh=mesh, in_specs=in_specs, out_specs=out_specs, check_vma=False)
```

profile of v0, /device:TPU:1, one launch (start us, length us, event | category | flops | bytes accessed | tf_op | source)
XLA Modules:
  0.0 302.1 jit_solution(13077538470099252400)
XLA Ops:
  6.5 0.7 all-gather.3.cloned.1.call-update
  7.3 0.0 reduce-scatter.5.cloned.1.call-start
  7.3 51.9 %all-gather.3.cloned.1.call-done = bf16[3584,512]{1,0:T(8,128)(2,1)} async-done(((bf16[896,512]{1,0:T(8,128)(2,1)}), bf16[3584,512]{1,0:T(8,128)(2,1)}) %all-gather.3.cloned.1.call-update) | async-done | bytes 3670032 | tf_op jit(solution)/shard_map/all_gather | solution.py:43
  59.2 9.0 %convolution_convert_fusion.1 = bf16[3584,896]{1,0:T(8,128)(2,1)} fusion(bf16[3584,512]{1,0:T(8,128)(2,1)} %all-gather.3.cloned.1.call-done, bf16[896,512]{1,0:T(8,128)(2,1)} %param.1), kind=kOutput, calls=%fused_computation.1 | convolution fusion | flops 3291545600 | bytes 11010048 | tf_op jit(solution)/shard_map/dot_general | solution.py:46
  68.2 0.0 reduce-scatter.5.cloned.1.call-update
  68.2 0.0 reduce-scatter.7.cloned.1.call-start
  68.2 20.7 %reduce-scatter.5.cloned.1.call-done = bf16[1792,896]{1,0:T(8,128)(2,1)} async-done(((bf16[3584,896]{1,0:T(8,128)(2,1)}), bf16[1792,896]{1,0:T(8,128)(2,1)}) %reduce-scatter.5.cloned.1.call-update) | async-done | bytes 3211280 | tf_op jit(solution)/shard_map/reduce_scatter | solution.py:17
  88.9 0.0 reduce-scatter.7.cloned.1.call-update
  88.9 0.0 reduce-scatter.9.cloned.1.call-start
  89.0 48.8 %reduce-scatter.7.cloned.1.call-done = bf16[224,896]{1,0:T(8,128)(2,1)} async-done(((bf16[1792,896]{1,0:T(8,128)(2,1)}), bf16[224,896]{1,0:T(8,128)(2,1)}) %reduce-scatter.7.cloned.1.call-update) | async-done | bytes 401424 | tf_op jit(solution)/shard_map/reduce_scatter | solution.py:17
  137.8 1.1 broadcast_in_dim.3
  139.0 21.5 %all_to_all.5 = bf16[4,224,896]{2,1,0:T(8,128)(2,1)S(1)} all-to-all(bf16[4,224,896]{2,1,0:T(8,128)(2,1)S(1)} %broadcast_in_dim.3), channel_id=1, replica_groups=mesh['layer'=4,'rep'=2,'row'=4,'col'=8] {'row'}, dimensions={0} | all-to-all | bytes 3211264 | tf_op jit(solution)/shard_map/all_to_all | solution.py:29
  160.5 0.1 copy.3
  160.6 4.9 %convolution_convert_fusion = bf16[3584,896]{1,0:T(8,128)(2,1)} fusion(bf16[224,3584]{1,0:T(8,128)(2,1)S(1)} %bitcast.9, bf16[224,896]{1,0:T(8,128)(2,1)S(1)} %copy-done), kind=kOutput, calls=%fused_computation | convolution fusion | flops 1441857536 | bytes 8429568 | tf_op jit(solution)/shard_map/dot_general | solution.py:37
  165.5 0.0 reduce-scatter.9.cloned.1.call-update
  165.5 0.0 reduce-scatter.11.cloned.1.call-start
  165.6 21.6 %reduce-scatter.9.cloned.1.call-done = bf16[1792,896]{1,0:T(8,128)(2,1)} async-done(((bf16[3584,896]{1,0:T(8,128)(2,1)}), bf16[1792,896]{1,0:T(8,128)(2,1)}) %reduce-scatter.9.cloned.1.call-update) | async-done | bytes 3211280 | tf_op jit(solution)/shard_map/reduce_scatter | solution.py:17
  187.1 0.0 reduce-scatter.11.cloned.1.call-update
  187.2 0.0 all-gather.5.cloned.1.call-start
  187.2 48.7 %reduce-scatter.11.cloned.1.call-done = bf16[224,896]{1,0:T(8,128)(2,1)} async-done(((bf16[1792,896]{1,0:T(8,128)(2,1)}), bf16[224,896]{1,0:T(8,128)(2,1)}) %reduce-scatter.11.cloned.1.call-update) | async-done | bytes 401424 | tf_op jit(solution)/shard_map/reduce_scatter | solution.py:17
  235.9 1.9 add_convert_fusion
  237.8 0.0 all-gather.5.cloned.1.call-update
  237.8 49.1 %all-gather.5.cloned.1.call-done = bf16[3584,896]{1,0:T(8,128)(2,1)} async-done(((bf16[224,896]{1,0:T(8,128)(2,1)}), bf16[3584,896]{1,0:T(8,128)(2,1)}) %all-gather.5.cloned.1.call-update) | async-done | bytes 6422544 | tf_op jit(solution)/shard_map/all_gather | solution.py:58
  287.0 8.3 %multiply_convert_fusion = bf16[896,512]{1,0:T(8,128)(2,1)} fusion(bf16[896,512]{1,0:T(8,128)(2,1)S(1)} %copy-done.1, bf16[3584,896]{1,0:T(8,128)(2,1)} %all-gather.5.cloned.1.call-done, bf16[3584,512]{1,0:T(8,128)(2,1)} %all-gather.3.cloned.1.call-done), kind=kOutput, calls=%fused_computation.2 | convolution fusion | flops 3290628096 | bytes 11927552 | tf_op jit(solution)/shard_map/dot_general | solution.py:37
  (5 shorter events, 0.0 us)
Async XLA Ops:
  6.5 52.6 %all-gather.3.cloned.1.call-start = ((), (), s32[]{:S(2)}) async-start(), calls=%async_computation.5 | async-start | bytes 4587520 | tf_op jit(solution)/shard_map/all_gather | solution.py:43
  7.3 81.7 %reduce-scatter.5.cloned.1.call-start = ((), (), s32[]{:S(2)}) async-start(), calls=%async_computation.6 | async-start | bytes 9633792 | tf_op jit(solution)/shard_map/reduce_scatter | solution.py:17
  68.2 69.6 %reduce-scatter.7.cloned.1.call-start = ((), (), s32[]{:S(2)}) async-start(), calls=%async_computation.7 | async-start | bytes 3612672 | tf_op jit(solution)/shard_map/reduce_scatter | solution.py:17
  88.9 98.2 %reduce-scatter.9.cloned.1.call-start = ((), (), s32[]{:S(2)}) async-start(), calls=%async_computation.8 | async-start | bytes 9633792 | tf_op jit(solution)/shard_map/reduce_scatter | solution.py:17
  138.9 21.7 %copy-start = (bf16[224,896]{1,0:T(8,128)(2,1)S(1)}, bf16[224,896]{1,0:T(8,128)(2,1)}, u32[]{:S(2)}) copy-start(bf16[224,896]{1,0:T(8,128)(2,1)} %reduce-scatter.7.cloned.1.call-done) | copy-start | bytes 1204228
  165.5 121.5 %copy-start.1 = (bf16[896,512]{1,0:T(8,128)(2,1)S(1)}, bf16[896,512]{1,0:T(8,128)(2,1)}, u32[]{:S(2)}) copy-start(bf16[896,512]{1,0:T(8,128)(2,1)} %param.1) | copy-start | bytes 2752516
  165.5 70.4 %reduce-scatter.11.cloned.1.call-start = ((), (), s32[]{:S(2)}) async-start(), calls=%async_computation.9 | async-start | bytes 3612672 | tf_op jit(solution)/shard_map/reduce_scatter | solution.py:17
  187.2 99.8 %all-gather.5.cloned.1.call-start = ((), (), s32[]{:S(2)}) async-start(), calls=%async_computation.10 | async-start | bytes 6823936 | tf_op jit(solution)/shard_map/all_gather | solution.py:58
Sparse Core Ops, SparseCore 0:
  9.1 49.9 all-gather.2
  68.3 20.5 reduce-scatter.4
  91.5 46.2 reduce-scatter.6
  165.6 21.4 reduce-scatter.8
  189.5 46.3 reduce-scatter.10
  238.0 48.9 all-gather.4
where the time goes:
time: 302 us
  waiting for transfers between devices  242 us (80%)
  matrix products  22.2 us (7%)
  blocking collectives  21.5 us (7%)
  between operations  13.5 us (4%)
    reduce_scatter x4, waiting for transfers between devices, summed_rows(): total = lax.psum_scatter(total, axis, scatter_dimension=0, tiled=True)  140 us
    all_gather x1, waiting for transfers between devices, local(): column_panel = lax.all_gather(iterate, 'row', axis=0, tiled=True)  51.9 us
    all_gather x1, waiting for transfers between devices, local(): lax.all_gather(combo_tile, ('rep', 'col'), axis=0, tiled=True)  49.1 us
    all_to_all x1, blocking collectives, from_everyone(): return lax.all_to_all(copies, axis, split_axis=0, concat_axis=0, tiled=True)  21.5 us
    dot_general x2, matrix products, contract_first(): lax.dot_general(left_side, right_side, (((0,), (0,)), ((), ())), preferre...  13.2 us
    dot_general x1, matrix products, local(): lax.dot_general(panel_rows, iterate, (((1,), (1,)), ((), ())), preferred_...  9 us
  transfers between devices with their start and end apart: 6, of which 6 were waited for; matrix products, arithmetic and copies ran while one was open for 0% of the time, Pallas kernels for 0%

commit v1 on v0

v1 whole, which is shorter than its diff:
```python
import functools

import jax
import jax.numpy as jnp
from jax import lax
from jax.experimental import pallas as pl
from jax.experimental.pallas import tpu as pltpu
from jax.sharding import PartitionSpec as P

COLS = 8192

coef_linear = 3.4445
coef_cubic = -4.775
coef_quintic = 2.0315
MESH = pl.DeviceIdType.MESH
f32 = jnp.float32
bf16 = jnp.bfloat16


def dot(left, right):
    return jnp.dot(left, right, preferred_element_type=f32)


def dot_t(left, right):
    return lax.dot_general(
        left, right, (((1,), (1,)), ((), ())), preferred_element_type=f32
    )


def kernel(nz, sizes, x_ref, o_ref, xo, xq, g, part, rl, rs, v, acc, ob, ssem, rsem, lsem):
    core = lax.axis_index("rep")
    r = lax.axis_index("row")
    z = lax.axis_index("col")
    rows, width = x_ref.shape
    strip = rows // nz
    far, near = nz // 2, nz // 2 - 1
    units = range(len(sizes))
    offs = [sum(sizes[:u]) for u in units]
    right = {"row": lax.rem(r + 1, 4)}
    left = {"row": lax.rem(r + 3, 4)}
    partner = {"rep": 1 - core}
    keys = {}

    def at_z(k):
        return lax.rem(z + (k % nz), nz)

    def chunk(u):
        return pl.ds(nz * offs[u], nz * sizes[u])

    def piece(u, d):
        return pl.ds(pl.multiple_of(nz * offs[u] + d * sizes[u], 16), sizes[u])

    def slot(u):
        return pl.ds(offs[u], sizes[u])

    def way(t, u):
        return 1 if (t + u) % 2 == 0 else -1

    def rel(t, c=core):
        return 3 * c if t == 0 else 2 - c

    def link(key, src, dst, dev):
        i = keys.setdefault(key, len(keys))
        return pltpu.make_async_remote_copy(
            src_ref=src, dst_ref=dst, send_sem=ssem.at[i], recv_sem=rsem.at[i],
            device_id=dev, device_id_type=MESH,
        )

    def hop(buf, key, d, u):
        return link(
            key, buf.at[0, chunk(u)], buf.at[3 if d > 0 else 1, chunk(u)],
            right if d > 0 else left,
        )

    def relay(buf, key, d, u):
        return link(
            key, buf.at[3 if d > 0 else 1, chunk(u)], buf.at[2, chunk(u)],
            right if d > 0 else left,
        )

    def desc(key, incoming=False):
        kind = key[0]
        if kind == "X":
            return hop(xo, key, key[1], key[2])
        if kind == "V":
            return hop(v, key, key[1], key[2])
        if kind == "F":
            return relay(xo, key, key[1], key[2])
        if kind == "W":
            return relay(v, key, key[1], key[2])
        if kind == "P":
            _, k, u = key
            return link(key, xo.at[k, chunk(u)], xq.at[k, chunk(u)], partner)
        if kind == "G":
            _, t, u = key
            k = rel(t, 1 - core) if incoming else rel(t)
            return link(key, g.at[k, chunk(u)], g.at[k, chunk(u)], partner)
        _, t, u, s = key
        w = way(t, u)
        if kind == "RL":
            src = part.at[t, piece(u, at_z(far * w))] if s == 0 else rl.at[t, s - 1, slot(u)]
            return link(key, src, rl.at[t, s, slot(u)], {"col": at_z(w)})
        if kind == "RS":
            src = part.at[t, piece(u, at_z(-near * w))] if s == 0 else rs.at[t, s - 1, slot(u)]
            return link(key, src, rs.at[t, s, slot(u)], {"col": at_z(-w)})
        step = s + 1 if incoming else s
        if kind == "AL":
            here = g.at[rel(t), piece(u, at_z(-step * w))]
            return link(key, here, here, {"col": at_z(w)})
        here = g.at[rel(t), piece(u, at_z(step * w))]
        return link(key, here, here, {"col": at_z(-w)})

    sent = []

    def send(*key):
        desc(key).start()
        sent.append(key)

    def take(*key):
        desc(key, True).wait_recv()

    def gram(t, u):
        k = rel(t)
        mine, his = xo[0, chunk(u)], xq[0, chunk(u)]

        def columns(at, n):
            there = pl.ds(at, n)
            part[t, chunk(u), there] = (
                dot_t(mine, xo[k, there]) + dot_t(his, xq[k, there])
            ).astype(bf16)

        wide = rows // 256

        @pl.loop(0, wide)
        def _(i):
            columns(pl.multiple_of(i * 256, 256), 256)

        if rows % 256:
            columns(wide * 256, rows % 256)

    def begin(t, u):
        gram(t, u)
        send("RL", t, u, 0)
        send("RS", t, u, 0)

    def plus(buf, t, u, s, d):
        buf[t, s, slot(u)] = (
            buf[t, s, slot(u)].astype(f32) + part[t, piece(u, d)].astype(f32)
        ).astype(bf16)

    def reduce_step(t, u, s):
        w = way(t, u)
        take("RL", t, u, s)
        if s < far - 1:
            plus(rl, t, u, s, at_z((far - 1 - s) * w))
            send("RL", t, u, s + 1)
        if s < near:
            take("RS", t, u, s)
            if s < near - 1:
                plus(rs, t, u, s, at_z(-(near - 1 - s) * w))
                send("RS", t, u, s + 1)
        if s == far - 1:
            g[rel(t), piece(u, z)] = (
                rl[t, far - 1, slot(u)].astype(f32)
                + rs[t, near - 1, slot(u)].astype(f32)
                + part[t, piece(u, z)].astype(f32)
            ).astype(bf16)
            send("AL", t, u, 0)
            send("AS", t, u, 0)

    def gather_step(t, u, s):
        take("AL", t, u, s)
        if s < far - 1:
            send("AL", t, u, s + 1)
        if s < near:
            take("AS", t, u, s)
            if s < near - 1:
                send("AS", t, u, s + 1)
        if s == far - 1:
            send("G", t, u)

    loads = [
        pltpu.make_async_copy(
            x_ref.at[pl.ds(d * strip + offs[u], sizes[u])],
            xo.at[0, pl.ds(nz * offs[u] + d * sizes[u], sizes[u])],
            lsem.at[u * nz + d],
        )
        for u in units
        for d in range(nz)
    ]
    for load in loads:
        load.start()
    barrier = pltpu.get_barrier_semaphore()
    for dev in (right, left, partner, {"col": at_z(1)}, {"col": at_z(-1)}):
        pl.semaphore_signal(barrier, inc=1, device_id=dev, device_id_type=MESH)
    pl.semaphore_wait(barrier, 5)
    for load in loads:
        load.wait()

    send("P", 0, 0)
    send("P", 0, 1)
    send("X", 1, 0)
    send("X", -1, 1)
    send("X", 1, 1)
    send("X", -1, 0)
    take("P", 0, 0)
    take("P", 0, 1)
    common = list(sent)

    def pass_on(share):
        take("X", 1, 0)
        send("F", 1, 0)
        take("X", -1, 1)
        send("F", -1, 1)
        if share:
            send("P", 3, 0)
            send("P", 1, 1)

    def rest_of_ones(share):
        take("X", 1, 1)
        take("X", -1, 0)
        if share:
            send("P", 3, 1)
            send("P", 1, 0)

    def twos(share):
        take("F", 1, 0)
        take("F", -1, 1)
        if share:
            send("P", 2, 0)
            send("P", 2, 1)

    sent.clear()

    @pl.when(core == 0)
    def _():
        for u in units:
            begin(0, u)
        for s in range(far):
            for u in units:
                reduce_step(0, u, s)
        pass_on(True)
        for s in range(far):
            for u in units:
                gather_step(0, u, s)
        rest_of_ones(True)
        twos(False)
        take("P", 2, 0)
        take("P", 2, 1)
        for u in units:
            begin(1, u)
        for s in range(far):
            for u in units:
                reduce_step(1, u, s)
        for s in range(far):
            for u in units:
                gather_step(1, u, s)

    zero_sent = list(sent)
    sent.clear()

    @pl.when(core == 1)
    def _():
        pass_on(False)
        rest_of_ones(False)
        for k in (3, 1):
            for u in units:
                take("P", k, u)
        for u in units:
            for t in (0, 1):
                begin(t, u)
        for s in range(far):
            if s == far // 2:
                twos(True)
            for u in units:
                for t in (0, 1):
                    reduce_step(t, u, s)
        for s in range(far):
            for u in units:
                for t in (0, 1):
                    gather_step(t, u, s)

    one_sent = list(sent)
    sent.clear()

    for u in units:
        take("G", 0, u)
        take("G", 1, u)
        here = acc.at[pl.ds(0, nz * sizes[u])]
        here[...] = coef_cubic * xo[0, chunk(u)].astype(f32)

        @pl.loop(0, 4)
        def _(k):
            here[...] += coef_quintic * dot(g[k, chunk(u)], xo[k])

        v[0, chunk(u)] = here[...].astype(bf16)
        send("V", 1, u)
        send("V", -1, u)

    half = rows // 2

    def apply(k):
        @pl.loop(0, 2)
        def _(i):
            part_rows = pl.ds(pl.multiple_of(i * half, half), half)
            acc[part_rows] += dot(g[k, part_rows], v[k])

    acc[...] = coef_linear * xo[0].astype(f32)
    apply(0)
    take("V", 1, 0)
    send("W", 1, 0)
    take("V", -1, 0)
    take("V", -1, 1)
    send("W", -1, 1)
    take("V", 1, 1)
    apply(3)
    apply(1)
    take("W", 1, 0)
    take("W", -1, 1)
    apply(2)
    scale = 0.2 * jnp.sqrt(f32(COLS))
    ob[...] = (scale * acc[...]).astype(bf16)
    stores = [
        pltpu.make_async_copy(
            ob.at[pl.ds(nz * offs[u] + d * sizes[u], sizes[u])],
            o_ref.at[pl.ds(d * strip + offs[u], sizes[u])],
            lsem.at[u * nz + d],
        )
        for u in units
        for d in range(nz)
    ]
    for store in stores:
        store.start()

    def drain(some):
        for key in some:
            desc(key).wait_send()

    drain(common + sent)

    @pl.when(core == 0)
    def _():
        drain(zero_sent)

    @pl.when(core == 1)
    def _():
        drain(one_sent)

    for store in stores:
        store.wait()


def local(nz, iterate):
    rows, width = iterate.shape
    strip = rows // nz
    first = -(-strip // 32) * 16
    sizes = (first, strip - first)
    far = nz // 2
    return pl.pallas_call(
        functools.partial(kernel, nz, sizes),
        out_shape=jax.ShapeDtypeStruct((rows, width), bf16),
        in_specs=[pl.BlockSpec(memory_space=pl.ANY)],
        out_specs=pl.BlockSpec(memory_space=pl.ANY),
        scratch_shapes=[
            pltpu.VMEM((4, rows, width), bf16),
            pltpu.VMEM((4, rows, width), bf16),
            pltpu.VMEM((4, rows, rows), bf16),
            pltpu.VMEM((2, rows, rows), bf16),
            pltpu.VMEM((2, far, strip, rows), bf16),
            pltpu.VMEM((2, far - 1, strip, rows), bf16),
            pltpu.VMEM((4, rows, width), bf16),
            pltpu.VMEM((rows, width), f32),
            pltpu.VMEM((rows, width), bf16),
            pltpu.SemaphoreType.DMA((96,)),
            pltpu.SemaphoreType.DMA((96,)),
            pltpu.SemaphoreType.DMA((2 * nz,)),
        ],
        compiler_params=pltpu.CompilerParams(
            collective_id=0, has_side_effects=True, vmem_limit_bytes=60 * 1024 * 1024
        ),
    )(iterate)


def solution(mesh):
    spec = P(("layer", "row"), ("rep", "col"))
    step = functools.partial(local, mesh.shape["col"])
    return jax.shard_map(step, mesh=mesh, in_specs=(spec,), out_specs=spec, check_vma=False)
```

time: 302 us -> 147 us (0.49)
  waiting for transfers between devices: 242 us -> 0 us
  Pallas kernels: 0 us -> 145 us
  matrix products: 22.2 us -> 0 us
  blocking collectives: 21.5 us -> 0 us
  between operations: 13.5 us -> 0.01 us
    pallas_call x0 -> x1, Pallas kernels: none -> 145 us  [local(): pl.pallas_call(functools.partial(kernel, nz, sizes), out_shape=jax.ShapeD...]
    reduce_scatter x4 -> x0, waiting for transfers between devices: 140 us -> none  [summed_rows(): total = lax.psum_scatter(total, axis, scatter_dimension=0, tiled=True)]
    all_gather x2 -> x0, waiting for transfers between devices: 101 us -> none  [the longest x1 51.9 us: local(): column_panel = lax.all_gather(iterate, 'row', axis=0, tiled=True)]
    dot_general x3 -> x0, matrix products: 22.2 us -> none  [the longest x2 13.2 us: contract_first(): lax.dot_general(left_side, right_side, (((0,), (0,)), ((), ())), preferre...]
    all_to_all x1 -> x0, blocking collectives: 21.5 us -> none  [from_everyone(): return lax.all_to_all(copies, axis, split_axis=0, concat_axis=0, tiled=True)]
  transfers between devices with their start and end apart: 6 -> 0, of which waited for: 6 -> 0; matrix products, arithmetic and copies ran while one was open for 0% -> 0% of each run, Pallas kernels for 0% -> 0%
where the time goes in v1:
time: 147 us
  Pallas kernels  145 us (99%)
  local copies, waits for them, and re-layouts  2.16 us (1%)
    pallas_call x1, Pallas kernels, local(): pl.pallas_call(functools.partial(kernel, nz, sizes), out_shape=jax.ShapeD...  145 us

profile of v1, /device:TPU:1, one launch (start us, length us, event | category | flops | bytes accessed | tf_op | source)
XLA Modules:
  0.0 147.2 jit_solution(1478100349792184439)
XLA Ops:
  0.0 145.0 %shard_map.17 = bf16[896,512]{1,0:T(8,128)(2,1)} custom-call(bf16[896,512]{1,0:T(8,128)(2,1)} %x_ref.1), custom_call_target="tpu_custom_call" | custom-call | tf_op jit(solution)/shard_map/pallas_call | solution.py:359
  145.0 2.2 %copy.3 = bf16[896,512]{1,0:T(8,128)(2,1)} copy(bf16[896,512]{1,0:T(8,128)(2,1)} %shard_map.17) | data formatting | bytes 1835008
